TPU v7x, 32 devices: a whole 2x2x4 slice. The times are simulated.
32 devices in a mesh: seq: 4 (over z), tp: 4 (over y, core), roll: 2 (over x).
Axes of the slice: x: 2, y: 2, z: 4, core: 2. Of those that a mesh axis runs over, the one named last changes fastest.
Arguments:
- hidden: bfloat16 [8, 3584], P('roll'), may hold values from -6 to 6
- norm_gain: bfloat16 [3584], replicated, may hold values from 0.25 to 1.75
- qkv_bias: bfloat16 [3072], replicated, may hold values from -20 to 20
- qkv_weight: bfloat16 [3584, 3072], P(('seq', 'tp', 'roll')), may hold values from -0.09375 to 0.09375
- out_weight: bfloat16 [3584, 2048], P(('seq', 'tp', 'roll')), may hold values from -0.125 to 0.125
- key_cache: bfloat16 [8, 16384, 512], P('roll', ('seq', 'tp')), may hold values from -16 to 16
- value_cache: bfloat16 [8, 16384, 512], P('roll', ('seq', 'tp')), may hold values from -16 to 16
- cache_len: int32 [8], P('roll'), may hold values from 8192 to 16384, as said below
- block_pos: int32 [8, 32], P('roll', ('seq', 'tp')), may hold values from 0 to 16383, as said below
Outputs:
- attended: bfloat16 [8, 3584], P('roll')
- fresh_kv: bfloat16 [8, 1024], P('roll')
- served_qkv: bfloat16 [3584, 3072], P(None, 'tp')
- served_out: bfloat16 [3584, 2048], P(None, 'tp')
Inputs may be any that keep to these rules, and one draw needn't show every extreme that they name: `cache_len`: in every draw one rollout has all 16384 positions cached. With i = cache_len[r] mod 8192, and c the 8192-position stretch that holds position cache_len[r]: block_pos[r, b] is i where block b lies in c, i + 8192 where it lies in a later stretch or in the stretch just before c, and 16383 elsewhere.
All inputs are finite; a program needn't handle non-finite values.
Results may differ from a plain program's by a relative error of at most 0.009.
Values may be sent and summed in bfloat16 or wider, within the bound.
A program may use at most 128 MiB of HBM per device.

v0:
```python
import jax
import jax.numpy as jnp
import numpy as np
from jax import lax
from jax.sharding import PartitionSpec as P

HQ = 16
KVH = 4
HD = 128
BLOCK = 512
STRETCH = 8192


rope_base = 10000000.0
norm_eps = 1e-06
floor_score = -1e30


def frequencies(width):
    half_width = width // 2
    exact = rope_base ** (-2.0 * np.arange(half_width) / width)
    octave = np.floor(np.log2(exact))
    quantum = 2.0 ** (8.0 - octave)
    return np.floor(exact * quantum) / quantum


def rotate(vectors, positions):
    half_width = vectors.shape[-1] // 2
    inverse = jnp.asarray(frequencies(vectors.shape[-1]), dtype=jnp.float32)
    angles = positions.astype(jnp.float32)[..., None] * inverse
    cosine = jnp.cos(angles)
    sine_part = jnp.sin(angles)
    front_half = vectors[..., :half_width]
    back_half = vectors[..., half_width:]
    return jnp.concatenate(
        [front_half * cosine - back_half * sine_part, back_half * cosine + front_half * sine_part],
        axis=-1,
    )


def arrange(columns, tp_count):
    lead = columns.shape[:-1]
    per_rank = HQ // tp_count
    query_part = columns[..., : HQ * HD].reshape(lead + (tp_count, per_rank * HD))
    key_part = jnp.repeat(
        columns[..., HQ * HD : (HQ + KVH) * HD].reshape(lead + (KVH, HD)), tp_count // KVH, axis=-2
    )
    value_part = jnp.repeat(
        columns[..., (HQ + KVH) * HD :].reshape(lead + (KVH, HD)), tp_count // KVH, axis=-2
    )
    return jnp.concatenate([query_part, key_part, value_part], axis=-1)


def normalize(row_block, norm_gain):
    wide_rows = row_block.astype(jnp.float32)
    scaled = wide_rows * lax.rsqrt(
        jnp.mean(wide_rows * wide_rows, axis=1, keepdims=True) + norm_eps
    )
    return (scaled * norm_gain.astype(jnp.float32)).astype(jnp.bfloat16)


def body(
    hidden,
    norm_gain,
    qkv_bias,
    qkv_weight,
    out_weight,
    key_cache,
    value_cache,
    cache_len,
    block_pos,
):
    tp_count = lax.axis_size("tp")
    tp_index = lax.axis_index("tp")
    head_cols = out_weight.shape[1]
    rollouts = hidden.shape[0]
    group_size = HQ // KVH
    score_scale = HD ** (-0.5)
    per_rank = HQ // tp_count
    served_width = (per_rank + 2) * HD
    head_width = head_cols // tp_count
    paired = (
        lax.all_gather(qkv_weight, "roll", axis=0, tiled=True),
        lax.all_gather(out_weight, "roll", axis=0, tiled=True),
    )
    pair_rows = paired[0].shape[0]
    qkv_blocks = arrange(paired[0], tp_count)
    out_blocks = paired[1].reshape(pair_rows, tp_count, head_width)
    traded = (
        lax.all_to_all(qkv_blocks, "tp", split_axis=1, concat_axis=0, tiled=True),
        lax.all_to_all(out_blocks, "tp", split_axis=1, concat_axis=0, tiled=True),
    )
    traded_qkv = traded[0].reshape(tp_count * pair_rows, served_width)
    traded_out = traded[1].reshape(tp_count * pair_rows, head_width)
    served_qkv, served_out = (
        lax.all_gather(traded_qkv, "seq", axis=0, tiled=True),
        lax.all_gather(traded_out, "seq", axis=0, tiled=True),
    )
    bias_wide = qkv_bias.astype(jnp.float32)
    normed = normalize(hidden, norm_gain)
    bias_grouped = arrange(bias_wide, tp_count)
    own_bias = lax.dynamic_slice_in_dim(bias_grouped, tp_index, 1, 0).reshape(served_width)
    local_cols = jnp.dot(normed, served_qkv, preferred_element_type=jnp.float32) + own_bias
    gathered = lax.all_gather(local_cols.astype(jnp.bfloat16), "tp", axis=1, tiled=True)
    grouped_cols = gathered.reshape(rollouts, tp_count, served_width)
    repeat_count = tp_count // KVH
    queries = grouped_cols[:, :, : per_rank * HD].reshape(rollouts, HQ, HD).astype(jnp.float32)
    new_keys = grouped_cols[:, ::repeat_count, per_rank * HD : (per_rank + 1) * HD].astype(
        jnp.float32
    )
    fresh_value = grouped_cols[:, ::repeat_count, (per_rank + 1) * HD :]
    intra_pos = cache_len % STRETCH
    fresh_key = rotate(new_keys, jnp.broadcast_to(intra_pos[:, None], (rollouts, KVH))).astype(
        jnp.bfloat16
    )
    self_query = rotate(queries, jnp.broadcast_to(intra_pos[:, None], (rollouts, HQ))).astype(
        jnp.bfloat16
    )
    self_score = score_scale * jnp.einsum(
        "rkgd,rkd->rkg",
        self_query.reshape(rollouts, KVH, group_size, HD),
        fresh_key,
        preferred_element_type=jnp.float32,
    )
    blocks = block_pos.shape[1]
    block_query = rotate(
        queries[:, None], jnp.broadcast_to(block_pos[:, :, None], (rollouts, blocks, HQ))
    ).astype(jnp.bfloat16)
    cached_keys = key_cache.reshape(rollouts, blocks, BLOCK, KVH, HD)
    cached_values = value_cache.reshape(rollouts, blocks, BLOCK, KVH, HD)
    scores = score_scale * jnp.einsum(
        "rbkgd,rbpkd->rkgbp",
        block_query.reshape(rollouts, blocks, KVH, group_size, HD),
        cached_keys,
        preferred_element_type=jnp.float32,
    )
    shard_start = lax.axis_index(("seq", "tp")) * key_cache.shape[1]
    positions = shard_start + jnp.arange(key_cache.shape[1], dtype=jnp.int32).reshape(blocks, BLOCK)
    valid_mask = (positions[None] < cache_len[:, None, None])[:, None, None]
    masked = jnp.where(valid_mask, scores, floor_score)
    local_max = jnp.max(masked, axis=(3, 4))
    weights = jnp.where(valid_mask, jnp.exp(masked - local_max[..., None, None]), 0.0)
    local_sum = jnp.sum(weights, axis=(3, 4))
    local_out = jnp.einsum(
        "rkgbp,rbpkd->rkgd",
        weights.astype(jnp.bfloat16),
        cached_values,
        preferred_element_type=jnp.float32,
    )
    total_max = lax.pmax(local_max, ("seq", "tp"))
    factor = jnp.exp(local_max - total_max)
    total_sum, total_out = lax.psum(
        (local_sum * factor, local_out * factor[..., None]), ("seq", "tp")
    )
    top_score = jnp.maximum(total_max, self_score)
    old_factor = jnp.exp(total_max - top_score)
    fresh_weight = jnp.exp(self_score - top_score)
    fresh_rounded = lax.optimization_barrier(fresh_weight.astype(jnp.bfloat16)).astype(jnp.float32)
    denominator = total_sum * old_factor + fresh_weight
    numerator = (
        total_out * old_factor[..., None]
        + fresh_rounded[..., None] * fresh_value.astype(jnp.float32)[:, :, None, :]
    )
    attention = (numerator / denominator[..., None]).reshape(rollouts, HQ * HD).astype(jnp.bfloat16)
    own_heads = lax.dynamic_slice_in_dim(attention, tp_index * head_width, head_width, 1)
    partial_out = lax.dot_general(
        own_heads, served_out, (((1,), (1,)), ((), ())), preferred_element_type=jnp.float32
    )
    attended = lax.psum(partial_out, "tp").astype(jnp.bfloat16)
    fresh_kv = jnp.concatenate(
        [fresh_key.reshape(rollouts, KVH * HD), fresh_value.reshape(rollouts, KVH * HD)], axis=1
    )
    return (attended, fresh_kv, served_qkv, served_out)


def solution(mesh):
    return jax.shard_map(
        body,
        mesh=mesh,
        in_specs=(
            P("roll", None),
            P(),
            P(),
            P(("seq", "tp", "roll"), None),
            P(("seq", "tp", "roll"), None),
            P("roll", ("seq", "tp"), None),
            P("roll", ("seq", "tp"), None),
            P("roll"),
            P("roll", ("seq", "tp")),
        ),
        out_specs=(P("roll", None), P("roll", None), P(None, "tp"), P(None, "tp")),
        check_vma=False,
    )
```

profile of v0, /device:TPU:0, one launch (start us, length us, event | category | flops | bytes accessed | tf_op | source)
XLA Modules:
  0.0 351.2 jit_solution(4346206779094288452)
XLA Ops:
  7.2 0.7 all-gather.4.cloned.1.call-update
  7.9 16.3 %all_gather.18 = bf16[224,2048]{1,0:T(8,128)(2,1)S(1)} all-gather(bf16[112,2048]{1,0:T(8,128)(2,1)} %param.16), channel_id=1, replica_groups=mesh['seq'=4,'tp'=4,'roll'=2] {'roll'}, dimensions={0}, use_global_device_ids=true | all-gather | bytes 1376256 | tf_op jit(solution)/shard_map/all_gather | solution.py:84
  24.3 16.2 %all_to_all.30 = bf16[224,4,512]{2,0,1:T(8,128)(2,1)} all-to-all(bf16[224,4,512]{2,0,1:T(8,128)(2,1)S(1)} %bitcast.64), channel_id=1, replica_groups=mesh['seq'=4,'tp'=4,'roll'=2] {'tp'}, dimensions={1} | all-to-all | bytes 1835008 | tf_op jit(solution)/shard_map/all_to_all | solution.py:91
  40.6 1.2 slice.93
  41.9 1.1 slice_bitcast_fusion.1
  43.0 0.1 copy_bitcast_fusion.2
  43.1 0.1 pad_maximum_fusion
  43.3 21.1 %all_to_all.31 = bf16[224,4,768]{2,0,1:T(8,128)(2,1)} all-to-all(bf16[224,4,768]{2,0,1:T(8,128)(2,1)S(1)} %pad_maximum_fusion), channel_id=1, replica_groups=mesh['seq'=4,'tp'=4,'roll'=2] {'tp'}, dimensions={1} | all-to-all | bytes 2752512 | tf_op jit(solution)/shard_map/all_to_all | solution.py:90
  64.5 0.1 copy.19
  64.6 6.9 %reshape.139 = bf16[4,2,512,4,128]{4,3,2,1,0:T(4,128)(2,1)} reshape(bf16[4,1024,512]{2,1,0:T(8,128)(2,1)} %param.17) | data formatting | bytes 8388608 | tf_op jit(solution)/shard_map/reshape | solution.py:129
  71.5 6.9 %reshape.140 = bf16[4,2,512,4,128]{4,3,2,1,0:T(4,128)(2,1)} reshape(bf16[4,1024,512]{2,1,0:T(8,128)(2,1)} %param.18) | data formatting | bytes 8388608 | tf_op jit(solution)/shard_map/reshape | solution.py:130
  78.5 0.1 fusion.34
  78.8 35.2 %all-gather.8.cloned.1.call-done = bf16[3584,512]{1,0:T(8,128)(2,1)} async-done(((bf16[896,512]{1,0:T(8,128)(2,1)}), bf16[3584,512]{1,0:T(8,128)(2,1)}) %all-gather.8.cloned.1.call-update) | async-done | bytes 3670032 | tf_op jit(solution)/shard_map/all_gather | solution.py:97
  114.0 102.5 %all-gather.6.cloned.1.call-done = bf16[3584,768]{1,0:T(8,128)(2,1)} async-done(((bf16[896,768]{1,0:T(8,128)(2,1)}), bf16[3584,768]{1,0:T(8,128)(2,1)}) %all-gather.6.cloned.1.call-update) | async-done | bytes 5505040 | tf_op jit(solution)/shard_map/all_gather | solution.py:96
  216.5 3.4 fusion.19
  219.9 5.2 %all_gather.17 = bf16[4,3072]{1,0:T(4,128)(2,1)S(1)} all-gather(bf16[4,768]{1,0:T(4,128)(2,1)S(1)} %fusion.19), channel_id=1, replica_groups=mesh['seq'=4,'tp'=4,'roll'=2] {'tp'}, dimensions={1}, use_global_device_ids=true | all-gather | bytes 30720 | tf_op jit(solution)/shard_map/all_gather | solution.py:104
  225.2 0.1 fusion.57
  225.4 0.1 fusion.80
  225.6 0.2 fusion.31
  225.8 3.5 fusion.76
  229.3 31.4 %pmax.7 = f32[4,4,4]{2,1,0:T(4,128)S(1)} all-reduce(f32[4,4,4]{2,1,0:T(4,128)S(1)} %get-tuple-element.26), channel_id=1, replica_groups=mesh['seq'=4,'tp'=4,'roll'=2] {'seq','tp'}, use_global_device_ids=true, to_apply=%region_2.3 | all-reduce | flops 64 | bytes 512 | tf_op jit(solution)/shard_map/pmax | solution.py:150
  260.8 0.3 fusion.20
  261.1 0.1 fusion.42
  261.2 3.0 fusion.16
  264.3 57.7 %all-reduce = (f32[4,4,4,128]{3,2,1,0:T(4,128)S(1)}, f32[4,4,4]{2,1,0:T(4,128)S(1)}) all-reduce(f32[4,4,4,128]{3,2,1,0:T(4,128)S(1)} %fusion.16, f32[4,4,4]{2,1,0:T(4,128)S(1)} %bitcast.72), channel_id=1, replica_groups=mesh['seq'=4,'tp'=4,'roll'=2] {'seq','tp'}, use_global_device_ids=true, to_apply=%region_3.4 | all-reduce | flops 8256 | bytes 66048 | tf_op jit(solution)/shard_map/psum | solution.py:152
  322.0 0.2 fusion.52
  322.2 0.1 fusion.48
  322.4 3.1 fusion.62
  325.4 11.3 %psum.23 = bf16[4,3584]{1,0:T(4,128)(2,1)} all-reduce(f32[4,3584]{1,0:T(4,128)S(1)} %fusion.62), channel_id=1, replica_groups=mesh['seq'=4,'tp'=4,'roll'=2] {'tp'}, use_global_device_ids=true, to_apply=%region_6.7 | all-reduce | flops 14336 | bytes 86016 | tf_op jit(solution)/shard_map/psum | solution.py:169
  336.7 0.6 pad_maximum_fusion.3
  337.3 5.5 %copy.62 = bf16[3584,768]{1,0:T(8,128)(2,1)} copy(bf16[3584,768]{1,0:T(8,128)(2,1)} %all-gather.6.cloned.1.call-done) | data formatting | bytes 11010048
  342.8 1.8 copy.63
  (46 shorter events, 0.8 us)
Async XLA Ops:
  7.2 33.4 %all-gather.4.cloned.1.call-start = ((), (), s32[]{:S(2)}) async-start(), calls=%async_computation.2 | async-start | bytes 2064384 | tf_op jit(solution)/shard_map/all_gather | solution.py:83
  7.9 106.1 %all-gather.8.cloned.1.call-start = ((), (), s32[]{:S(2)}) async-start(), calls=%async_computation.4 | async-start | bytes 4587520 | tf_op jit(solution)/shard_map/all_gather | solution.py:97
  40.5 176.0 %all-gather.6.cloned.1.call-start = ((), (), s32[]{:S(2)}) async-start(), calls=%async_computation.3 | async-start | bytes 6881280 | tf_op jit(solution)/shard_map/all_gather | solution.py:96
  43.1 21.3 %copy-start.2 = (bf16[3072]{0:T(1024)(128)(2,1)S(1)}, bf16[3072]{0:T(1024)(128)(2,1)}, u32[]{:S(2)}) copy-start(bf16[3072]{0:T(1024)(128)(2,1)} %param.14) | copy-start | bytes 18436
  43.1 21.3 %copy-start.3 = (bf16[3584]{0:T(1024)(128)(2,1)S(1)}, bf16[3584]{0:T(1024)(128)(2,1)}, u32[]{:S(2)}) copy-start(bf16[3584]{0:T(1024)(128)(2,1)} %param.13) | copy-start | bytes 21508
  43.1 21.4 %copy-start.5 = (s32[4,2]{0,1:T(2,128)S(1)}, s32[4,2]{0,1:T(2,128)}, u32[]{:S(2)}) copy-start(s32[4,2]{0,1:T(2,128)} %param.20) | copy-start | bytes 100
  71.5 7.0 %copy-start.1 = (bf16[4,3584]{1,0:T(4,128)(2,1)S(1)}, bf16[4,3584]{1,0:T(4,128)(2,1)}, u32[]{:S(2)}) copy-start(bf16[4,3584]{1,0:T(4,128)(2,1)} %param.12) | copy-start | bytes 86020
  71.5 7.1 %copy-start.6 = (s32[4]{0:T(128)S(1)}, s32[4]{0:T(128)}, u32[]{:S(2)}) copy-start(s32[4]{0:T(128)} %param.19) | copy-start | bytes 52
  78.4 146.8 %copy-start.4 = (f32[64]{0:T(128)S(1)}, f32[64]{0:T(128)}, u32[]{:S(2)}) copy-start(f32[64]{0:T(128)} %constant.50.clone) | copy-start | bytes 772
  337.3 5.5 %copy-start = (bf16[3584,512]{1,0:T(8,128)(2,1)S(1)}, bf16[3584,512]{1,0:T(8,128)(2,1)}, u32[]{:S(2)}) copy-start(bf16[3584,512]{1,0:T(8,128)(2,1)} %all-gather.8.cloned.1.call-done) | copy-start | bytes 11010052
Sparse Core Ops, SparseCore 0:
  9.5 27.7 all-gather.3
  40.7 73.2 all-gather.7
  115.5 100.9 all-gather.5
where the time goes:
time: 352 us; the launch traced here: 351 us
  blocking collectives  159 us (45%)
  waiting for transfers between devices  138 us (39%)
  local copies, waits for them, and re-layouts  24 us (7%)
  between operations  14 us (4%)
  matrix products  13.2 us (4%)
    all_gather x1, waiting for transfers between devices, body(): lax.all_gather(traded_qkv, 'seq', axis=0, tiled=True)  103 us
    psum x1, blocking collectives, body(): lax.psum((local_sum * factor, local_out * factor[..., None]), ('seq', 'tp'))  57.7 us
    all_gather x1, waiting for transfers between devices, body(): lax.all_gather(traded_out, 'seq', axis=0, tiled=True)  35.2 us
    pmax x1, blocking collectives, body(): total_max = lax.pmax(local_max, ('seq', 'tp'))  31.4 us
    all_to_all x1, blocking collectives, body(): lax.all_to_all(qkv_blocks, 'tp', split_axis=1, concat_axis=0, tiled=True)  21.1 us
    all_gather x1, blocking collectives, body(): lax.all_gather(out_weight, 'roll', axis=0, tiled=True)  16.3 us
    all_to_all x1, blocking collectives, body(): lax.all_to_all(out_blocks, 'tp', split_axis=1, concat_axis=0, tiled=True)  16.2 us
    psum x1, blocking collectives, body(): attended = lax.psum(partial_out, 'tp').astype(jnp.bfloat16)  11.3 us
  transfers between devices with their start and end apart: 3, of which 2 were waited for; matrix products, arithmetic and copies ran while one was open for 5% of the time, Pallas kernels for 0%

commit v1 on v0

v1 whole, which is shorter than its diff:
```python
import functools

import jax
import jax.numpy as jnp
import numpy as np
from jax import lax
from jax.experimental import pallas as pl
from jax.experimental.pallas import tpu as pltpu
from jax.sharding import PartitionSpec as P

HQ = 16
KVH = 4
HD = 128
GROUP = HQ // KVH
BLOCK = 512
STRETCH = 8192
LANES = 128
SUB = 8

MESH = pl.DeviceIdType.MESH
rope_base = 10000000.0
norm_eps = 1e-06
floor_score = -1e30


def frequencies(width):
    half_width = width // 2
    exact = rope_base ** (-2.0 * np.arange(half_width) / width)
    octave = np.floor(np.log2(exact))
    quantum = 2.0 ** (8.0 - octave)
    return np.floor(exact * quantum) / quantum


def kernel(
    Z, T, X, nr, nb,
    nv_ref, norm_ref, cos_ref, sin_ref, bias_ref, wq_hbm, wo_hbm, k_hbm, v_hbm,
    sq, so, aout_ref, fkv_ref,
    wq, wo, kbuf, vbuf,
    nbuf, pq, qred, qmine, qall, part, pred, attm, att, proj, gat,
    loc_sem, kv_sem, own_sem,
    a_send, a_recv, up_send, dn_send, z_recv, x_send, x_recv,
    n_send, n_recv, d1_send, d1_recv, d2_send, d2_recv, d3_send, d3_recv,
    d4_send, d4_recv, d5_send, d5_recv,
):
    z, tp, x = lax.axis_index("seq"), lax.axis_index("tp"), lax.axis_index("roll")
    ND = Z * T * X
    NG = Z * T
    me = (z * T + tp) * X + x
    gi = z * T + tp
    rows = wq.shape[0]
    per = HQ // T
    QT = (HQ + 2 * KVH)
    NC = nr * KVH

    def coords(i):
        return (lax.div(i, T * X), lax.rem(lax.div(i, X), T), lax.rem(i, X))

    def remote(src, dst, ss, rs, dev):
        return pltpu.make_async_remote_copy(
            src_ref=src, dst_ref=dst, send_sem=ss, recv_sem=rs, device_id=dev, device_id_type=MESH
        )

    lq = pltpu.make_async_copy(wq_hbm, wq, loc_sem.at[0])
    lo = pltpu.make_async_copy(wo_hbm, wo, loc_sem.at[1])
    lk = pltpu.make_async_copy(k_hbm, kbuf, kv_sem.at[0])
    lv = pltpu.make_async_copy(v_hbm, vbuf, kv_sem.at[1])
    lq.start()
    lo.start()
    lk.start()
    lv.start()

    barrier = pltpu.get_barrier_semaphore()

    def greet(i, c):
        other = lax.rem(me + i, ND)
        pl.semaphore_signal(barrier, inc=1, device_id=coords(other), device_id_type=MESH)
        return c

    lax.fori_loop(1, ND, greet, 0)
    pl.semaphore_wait(barrier, ND - 1)

    def norm_copy(dx):
        ox = lax.rem(x + dx, X)
        return remote(norm_ref.at[ox], nbuf.at[x], n_send.at[dx - 1], n_recv.at[x], (z, tp, ox))

    for dx in range(1, X):
        norm_copy(dx).start()

    def pieces(t):
        kv = lax.div(t * KVH, T)
        yield wq.at[:, pl.ds(pl.multiple_of(t * per * HD, LANES), per * HD)], 0, per * HD
        yield wq.at[:, pl.ds(pl.multiple_of((HQ + kv) * HD, LANES), HD)], per * HD, HD
        yield wq.at[:, pl.ds(pl.multiple_of((HQ + KVH + kv) * HD, LANES), HD)], (per + 1) * HD, HD

    def out_piece(t):
        return wo.at[:, pl.ds(pl.multiple_of(t * per * HD, LANES), per * HD)]

    lq.wait()
    lo.wait()
    for dt in list(range(2, T)) + [1]:
        ot = lax.rem(tp + dt, T)
        for src, lo_col, width in pieces(ot):
            remote(src, sq.at[z, tp, x, :, pl.ds(lo_col, width)], a_send.at[dt, 0], a_recv.at[tp, 0], (z, ot, x)).start()
        remote(out_piece(ot), so.at[z, tp, x], a_send.at[dt, 1], a_recv.at[tp, 1], (z, ot, x)).start()
    for src, lo_col, width in pieces(tp):
        pltpu.make_async_copy(src, sq.at[z, tp, x, :, pl.ds(lo_col, width)], own_sem.at[0]).start()
    pltpu.make_async_copy(out_piece(tp), so.at[z, tp, x], own_sem.at[1]).start()

    def wait_local(ref, sem):
        pltpu.make_async_copy(ref, ref, sem).wait()

    both = ((0, sq), (1, so))

    def up(zo, s, j, ref):
        return remote(ref.at[zo, s, x], ref.at[zo, s, x], up_send.at[zo, s, j], z_recv.at[zo, s, j], (z + 1, tp, x))

    def down(zo, s, j, ref):
        return remote(ref.at[zo, s, x], ref.at[zo, s, x], dn_send.at[zo, s, j], z_recv.at[zo, s, j], (z - 1, tp, x))

    def cross(dx, zo, s, j, ref):
        ox = lax.rem(x + dx, X)
        return remote(
            ref.at[zo, s, x], ref.at[zo, s, x], x_send.at[dx - 1, zo, s, j], x_recv.at[x, zo, s, j], (z, tp, ox)
        )

    def spread_own(s):
        for j, ref in both:
            @pl.when(z + 1 < Z)
            def _():
                up(z, s, j, ref).start()

            @pl.when(z > 0)
            def _():
                down(z, s, j, ref).start()

            for dx in range(1, X):
                cross(dx, z, s, j, ref).start()

    def own_piece(dt):
        s = lax.rem(tp + T - dt, T)
        for j, ref in both:
            wait_local(ref.at[z, s, x], a_recv.at[s, j])
        spread_own(s)

    def pass_on(k, i):
        s = lax.rem(tp + i, T)

        @pl.when(z >= k)
        def _():
            for j, ref in both:
                wait_local(ref.at[z - k, s, x], z_recv.at[z - k, s, j])
                for dx in range(1, X):
                    cross(dx, z - k, s, j, ref).start()

                @pl.when(z + 1 < Z)
                def _():
                    up(z - k, s, j, ref).start()

        @pl.when(z + k < Z)
        def _():
            for j, ref in both:
                wait_local(ref.at[z + k, s, x], z_recv.at[z + k, s, j])
                for dx in range(1, X):
                    cross(dx, z + k, s, j, ref).start()

                @pl.when(z > 0)
                def _():
                    down(z + k, s, j, ref).start()

    lhs = norm_ref[x]
    for dx in range(1, X):
        ox = lax.rem(x + dx, X)
        wait_local(nbuf.at[ox], n_recv.at[ox])
        lhs = lhs + nbuf[ox]
    lhs = lhs[:, :rows].astype(jnp.bfloat16)
    for j in range(QT):
        pq[j] = jnp.dot(lhs, wq[:, j * HD:(j + 1) * HD], preferred_element_type=jnp.float32)

    def to_all(count, first, src_of, dst, ss, rs):
        def step(i, c):
            j = lax.rem(first + i, count)

            @pl.when(j != me)
            def _():
                remote(src_of(j), dst, ss, rs, coords(j)).start()

            @pl.when(j == me)
            def _():
                pltpu.make_async_copy(src_of(j), dst, rs).start()

            return c

        lax.fori_loop(0, count, step, 0)

    def drain(count, own, buf, ss):
        @pl.when(own < count)
        def _():
            wait_local(buf.at[pl.ds(0, count - 1)], ss)

        @pl.when(own >= count)
        def _():
            wait_local(buf.at[pl.ds(0, count)], ss)

    to_all(QT, lax.rem(me, QT), lambda j: pq.at[j], qred.at[me], d1_send, d1_recv)
    for j, ref in both:
        wait_local(ref.at[z, tp, x], own_sem.at[j])
    spread_own(tp)

    @pl.when(me < QT)
    def _():
        wait_local(qred, d1_recv)
        total = jnp.sum(qred[...], axis=0) + bias_ref[me]
        qmine[...] = total.astype(jnp.bfloat16).astype(jnp.float32)
        to_all(ND, me, lambda j: qmine, qall.at[me], d2_send, d2_recv)

    for dt in (1, 2):
        if dt < T:
            own_piece(dt)
    wait_local(qall, d2_recv)

    def turn(v, i):
        return v * cos_ref[i:i + 1, :] + pltpu.roll(v, HD // 2, 1) * sin_ref[i:i + 1, :]

    lk.wait()
    lv.wait()
    scale = HD ** (-0.5)
    sub3 = lax.broadcasted_iota(jnp.int32, (QT, SUB, LANES), 1)
    headrow = lax.broadcasted_iota(jnp.int32, (HQ, KVH * HD), 0) // GROUP
    headlane = lax.broadcasted_iota(jnp.int32, (HQ, KVH * HD), 1) // HD
    diag = headrow == headlane
    rowg = lax.broadcasted_iota(jnp.int32, (HQ, HD), 0) // GROUP
    lane = lax.broadcasted_iota(jnp.int32, (HQ, HD), 1)
    pos = lax.broadcasted_iota(jnp.int32, (HQ, BLOCK), 1)
    first_dev = gi == 0
    everything = qall[...]

    def per_head(v):
        out = jnp.zeros((HQ, HD), jnp.float32)
        for g in range(KVH):
            out = jnp.where(rowg == g, v[g:g + 1, :], out)
        return out

    for r in range(nr):
        mine = jnp.sum(jnp.where(sub3 == x * nr + r, everything, 0.0), axis=1)
        q = mine[:HQ]
        fk = turn(mine[HQ:HQ + KVH], r * (nb + 1) + nb).astype(jnp.bfloat16)
        fv = mine[HQ + KVH:]
        fkv_ref[r, :KVH, :] = fk.astype(jnp.float32)
        fkv_ref[r, KVH:, :] = fv
        sqy = turn(q, r * (nb + 1) + nb).astype(jnp.bfloat16).astype(jnp.float32)
        own = scale * jnp.sum(sqy * per_head(fk.astype(jnp.float32)), axis=1, keepdims=True)
        own = jnp.where(first_dev, own, floor_score)
        scores = []
        for b in range(nb):
            bq = turn(q, r * (nb + 1) + b)
            wide = jnp.where(diag, jnp.concatenate([bq] * KVH, axis=1), 0.0).astype(jnp.bfloat16)
            s = scale * lax.dot_general(
                wide, kbuf[r, b * BLOCK:(b + 1) * BLOCK, :], (((1,), (1,)), ((), ())),
                preferred_element_type=jnp.float32,
            )
            scores.append(jnp.where(pos < nv_ref[r * nb + b], s, floor_score))
        top = own
        for s in scores:
            top = jnp.maximum(top, jnp.max(s, axis=1, keepdims=True))
        w_own = jnp.where(first_dev, jnp.exp(own - top), 0.0)
        den = w_own
        acc = jnp.zeros((HQ, KVH * HD), jnp.float32)
        for b in range(nb):
            w = jnp.where(pos < nv_ref[r * nb + b], jnp.exp(scores[b] - top), 0.0)
            den = den + jnp.sum(w, axis=1, keepdims=True)
            acc = acc + jnp.dot(
                w.astype(jnp.bfloat16), vbuf[r, b * BLOCK:(b + 1) * BLOCK, :], preferred_element_type=jnp.float32
            )
        o = w_own.astype(jnp.bfloat16).astype(jnp.float32) * per_head(fv)
        for g in range(KVH):
            o = o + jnp.where(rowg == g, acc[:, g * HD:(g + 1) * HD], 0.0)
        stat = jnp.where(lane < HD // 2, top, den)
        for g in range(KVH):
            part[r * KVH + g] = jnp.concatenate(
                [o[g * GROUP:(g + 1) * GROUP], stat[g * GROUP:(g + 1) * GROUP]], axis=0
            )

    def to_group(i, c):
        j = lax.rem(gi + i, NC)

        @pl.when(j != gi)
        def _():
            remote(part.at[j], pred.at[gi], d3_send, d3_recv, (lax.div(j, T), lax.rem(j, T), x)).start()

        @pl.when(j == gi)
        def _():
            pltpu.make_async_copy(part.at[j], pred.at[gi], d3_recv).start()

        return c

    lax.fori_loop(0, NC, to_group, 0)

    for dt in range(3, T):
        own_piece(dt)

    @pl.when(gi < NC)
    def _():
        wait_local(pred, d3_recv)
        tiles = pred[...]
        o = tiles[:, :GROUP, :]
        m = tiles[:, GROUP:, 0:1]
        l = tiles[:, GROUP:, HD // 2:HD // 2 + 1]
        f = jnp.exp(m - jnp.max(m, axis=0, keepdims=True))
        val = jnp.sum(o * f, axis=0) / jnp.sum(l * f, axis=0)
        val = val.astype(jnp.bfloat16).astype(jnp.float32)
        attm[...] = jnp.concatenate([val, jnp.zeros_like(val)], axis=0)
        to_all(ND, me, lambda j: attm, att.at[x * NC + gi], d4_send, d4_recv)

    for i in range(T):
        pass_on(1, i)
    wait_local(att, d4_recv)

    nrt = nr * X
    prow = lax.broadcasted_iota(jnp.int32, (nrt * SUB, GROUP * HD), 0) % SUB
    plane = lax.broadcasted_iota(jnp.int32, (nrt * SUB, GROUP * HD), 1) // HD
    acc = jnp.zeros((nrt * SUB, rows), jnp.float32)
    for g in range(KVH):
        a = jnp.concatenate([att[i * KVH + g] for i in range(nrt)], axis=0)
        wide = jnp.where(prow == plane, jnp.concatenate([a] * GROUP, axis=1), 0.0).astype(jnp.bfloat16)
        acc = acc + lax.dot_general(
            wide, wo[:, g * GROUP * HD:(g + 1) * GROUP * HD], (((1,), (1,)), ((), ())),
            preferred_element_type=jnp.float32,
        )
    proj[...] = jnp.zeros_like(proj)
    for i in range(nrt):
        proj[i:i + 1, :rows] = jnp.sum(acc[i * SUB:(i + 1) * SUB], axis=0, keepdims=True)
    to_all(ND, me, lambda j: proj, gat.at[me], d5_send, d5_recv)

    for k in range(2, Z):
        for i in range(T):
            pass_on(k, i)

    wait_local(gat, d5_recv)
    aout_ref[...] = gat[...]

    for dx in range(1, X):
        norm_copy(dx).wait_send()
    drain(QT, me, pq, d1_send)

    @pl.when(me < QT)
    def _():
        drain(ND, me, gat, d2_send)

    drain(NC, gi, part, d3_send)

    @pl.when(gi < NC)
    def _():
        drain(ND, me, gat, d4_send)

    drain(ND, me, gat, d5_send)
    for dt in range(1, T):
        for j, ref in both:
            wait_local(ref.at[z, tp, x], a_send.at[dt, j])

    def finish(zs, c):
        zo, s = lax.div(zs, T), lax.rem(zs, T)
        for j, ref in both:
            piece = ref.at[zo, s, x]

            @pl.when((zo <= z) & (z + 1 < Z))
            def _():
                wait_local(piece, up_send.at[zo, s, j])

            @pl.when((zo >= z) & (z > 0))
            def _():
                wait_local(piece, dn_send.at[zo, s, j])

            for dx in range(1, X):
                wait_local(piece, x_send.at[dx - 1, zo, s, j])
                ox = lax.rem(x + dx, X)
                wait_local(ref.at[zo, s, ox], x_recv.at[ox, zo, s, j])
        return c

    lax.fori_loop(0, Z * T, finish, 0)


def make_body(Z, T, X):
    def body(hidden, norm_gain, qkv_bias, qkv_weight, out_weight, key_cache, value_cache, cache_len, block_pos):
        z, tp, x = lax.axis_index("seq"), lax.axis_index("tp"), lax.axis_index("roll")
        nr, D = hidden.shape
        nb = block_pos.shape[1]
        rows = qkv_weight.shape[0]
        per = HQ // T
        SC, HW = (per + 2) * HD, per * HD
        ND, NG, NC, QT = Z * T * X, Z * T, nr * KVH, HQ + 2 * KVH
        wide_rows = hidden.astype(jnp.float32)
        scaled = wide_rows * lax.rsqrt(jnp.mean(wide_rows * wide_rows, axis=1, keepdims=True) + norm_eps)
        normed = (scaled * norm_gain.astype(jnp.float32)).astype(jnp.bfloat16).astype(jnp.float32)
        blocks = lax.dynamic_slice_in_dim(normed, (z * T + tp) * X * rows, X * rows, 1)
        blocks = blocks.reshape(nr, X, rows).transpose(1, 0, 2)
        blocks = jnp.pad(blocks, ((0, 0), (0, 0), (0, LANES - rows)))
        slot = (jnp.arange(X) == x).astype(jnp.float32)
        blocks = (slot[None, :, None, None] * blocks[:, None]).reshape(X, X * nr, LANES)
        intra = cache_len % STRETCH
        pos = jnp.concatenate([block_pos, intra[:, None]], axis=1).reshape(-1)
        ang = pos.astype(jnp.float32)[:, None] * jnp.asarray(frequencies(HD), dtype=jnp.float32)
        cosine, sine = jnp.cos(ang), jnp.sin(ang)
        cos2 = jnp.concatenate([cosine, cosine], axis=1)
        sin2 = jnp.concatenate([-sine, sine], axis=1)
        start = (z * T + tp) * key_cache.shape[1]
        nv = (cache_len[:, None] - start - BLOCK * jnp.arange(nb, dtype=jnp.int32)[None]).reshape(-1)
        bias = qkv_bias.astype(jnp.float32).reshape(QT, 1, HD)
        vm = pl.BlockSpec(memory_space=pltpu.VMEM)
        anys = pl.BlockSpec(memory_space=pl.ANY)
        dma = pltpu.SemaphoreType.DMA
        f32, bf = jnp.float32, jnp.bfloat16
        tile = (SUB, LANES)
        sq, so, gat, fkv = pl.pallas_call(
            functools.partial(kernel, Z, T, X, nr, nb),
            out_shape=(
                jax.ShapeDtypeStruct((Z, T, X, rows, SC), bf),
                jax.ShapeDtypeStruct((Z, T, X, rows, HW), bf),
                jax.ShapeDtypeStruct((ND,) + tile, f32),
                jax.ShapeDtypeStruct((nr, 2 * KVH, HD), f32),
            ),
            in_specs=[pl.BlockSpec(memory_space=pltpu.SMEM)] + [vm] * 4 + [anys] * 4,
            out_specs=(anys, anys, vm, vm),
            scratch_shapes=[
                pltpu.VMEM(qkv_weight.shape, bf),
                pltpu.VMEM(out_weight.shape, bf),
                pltpu.VMEM(key_cache.shape, bf),
                pltpu.VMEM(value_cache.shape, bf),
                pltpu.VMEM((X,) + tile, f32),
                pltpu.VMEM((QT,) + tile, f32),
                pltpu.VMEM((ND,) + tile, f32),
                pltpu.VMEM(tile, f32),
                pltpu.VMEM((QT,) + tile, f32),
                pltpu.VMEM((NC,) + tile, f32),
                pltpu.VMEM((NG,) + tile, f32),
                pltpu.VMEM(tile, f32),
                pltpu.VMEM((X * NC,) + tile, f32),
                pltpu.VMEM(tile, f32),
                pltpu.VMEM((ND,) + tile, f32),
                dma((2,)), dma((2,)), dma((2,)),
                dma((T, 2)), dma((T, 2)),
                dma((Z, T, 2)), dma((Z, T, 2)), dma((Z, T, 2)),
                dma((X - 1, Z, T, 2)), dma((X, Z, T, 2)),
                dma((X - 1,)), dma((X,)),
            ] + [dma] * 10,
            compiler_params=pltpu.CompilerParams(
                collective_id=0, has_side_effects=True, vmem_limit_bytes=48 * 1024 * 1024
            ),
        )(nv, blocks, cos2, sin2, bias, qkv_weight, out_weight, key_cache, value_cache)
        mine = lax.dynamic_slice_in_dim(gat, x * nr, nr, 1)[:, :, :rows]
        attended = mine.transpose(1, 0, 2).reshape(nr, D).astype(bf)
        fresh_kv = fkv.reshape(nr, 2 * KVH * HD).astype(bf)
        return attended, fresh_kv, sq.reshape(D, SC), so.reshape(D, HW)

    return body


def solution(mesh):
    return jax.shard_map(
        make_body(mesh.shape["seq"], mesh.shape["tp"], mesh.shape["roll"]),
        mesh=mesh,
        in_specs=(
            P("roll", None),
            P(),
            P(),
            P(("seq", "tp", "roll"), None),
            P(("seq", "tp", "roll"), None),
            P("roll", ("seq", "tp"), None),
            P("roll", ("seq", "tp"), None),
            P("roll"),
            P("roll", ("seq", "tp")),
        ),
        out_specs=(P("roll", None), P("roll", None), P(None, "tp"), P(None, "tp")),
        check_vma=False,
    )
```

time: 352 us -> 144 us (0.41)
  blocking collectives: 159 us -> 0 us
  waiting for transfers between devices: 138 us -> 0 us
  Pallas kernels: 0 us -> 124 us
  between operations: 14 us -> 0.69 us
  matrix products: 13.2 us -> 0 us
  local copies, waits for them, and re-layouts: 24 us -> 13.9 us
    all_gather x3 -> x0, waiting for transfers between devices: 138 us -> none  [the longest x1 103 us: body(): lax.all_gather(traded_qkv, 'seq', axis=0, tiled=True)]
    pallas_call x0 -> x1, Pallas kernels: none -> 124 us  [body(): pl.pallas_call(functools.partial(kernel, Z, T, X, nr, nb), out_shape=(jax...]
    psum x2 -> x0, blocking collectives: 69 us -> none  [the longest x1 57.7 us: body(): lax.psum((local_sum * factor, local_out * factor[..., None]), ('seq', 'tp'))]
    all_to_all x2 -> x0, blocking collectives: 37.3 us -> none  [the longest x1 21.1 us: body(): lax.all_to_all(qkv_blocks, 'tp', split_axis=1, concat_axis=0, tiled=True)]
    pmax x1 -> x0, blocking collectives: 31.4 us -> none  [body(): total_max = lax.pmax(local_max, ('seq', 'tp'))]
    all_gather x2 -> x0, blocking collectives: 21.5 us -> none  [the longest x1 16.3 us: body(): lax.all_gather(out_weight, 'roll', axis=0, tiled=True)]
    reshape x5 -> x1, local copies, waits for them, and re-layouts: 14 us -> 0.09 us  [body(): blocks = blocks.reshape(nr, X, rows).transpose(1, 0, 2)]
    dot_general x5 -> x0, matrix products: 13.2 us -> none  [the longest x1 3.51 us: body(): jnp.einsum('rbkgd,rbpkd->rkgbp', block_query.reshape(rollouts, blocks, KV...]
  transfers between devices with their start and end apart: 3 -> 0, of which waited for: 2 -> 0; matrix products, arithmetic and copies ran while one was open for 5% -> 0% of each run, Pallas kernels for 0% -> 0%
where the time goes in v1:
time: 144 us; the launch traced here: 143 us
  Pallas kernels  124 us (86%)
  local copies, waits for them, and re-layouts  13.9 us (10%)
  other arithmetic  4.79 us (3%)
    pallas_call x1, Pallas kernels, body(): pl.pallas_call(functools.partial(kernel, Z, T, X, nr, nb), out_shape=(jax...  124 us
    unnamed x12, local copies, waits for them, and re-layouts  11.9 us

profile of v1, /device:TPU:0, one launch (start us, length us, event | category | flops | bytes accessed | tf_op | source)
XLA Modules:
  0.0 143.2 jit_solution(7055409827872970269)
XLA Ops:
  0.6 0.1 mul.77
  0.7 0.1 mul.78
  0.8 0.9 multiply_reduce_fusion
  1.7 0.7 fusion.5
  2.4 0.8 dynamic-slice
  3.1 0.7 add_convert_fusion
  3.8 0.1 copy.16
  3.9 0.1 convert_element_type.51
  4.0 0.1 broadcast_subtract_fusion
  4.1 0.1 sub.29.nv_ref
  4.2 0.7 reshape.68
  4.9 0.8 fusion.3
  5.6 0.1 pad_maximum_fusion
  5.7 0.8 convert_element_type.46
  6.5 0.1 fusion.4
  6.6 0.1 reshape.63
  6.7 0.1 broadcast_multiply_fusion.norm_ref
  6.7 0.0 copy-start.2
  6.7 1.1 copy-done.2
  7.8 0.0 copy-start.3
  7.8 1.0 copy-done.3
  8.9 123.7 %shard_map.129 = (bf16[4,4,2,112,768]{4,3,2,1,0:T(8,128)(2,1)}, bf16[4,4,2,112,512]{4,3,2,1,0:T(8,128)(2,1)S(1)}, f32[32,8,128]{2,1,0:T(8,128)S(1)}, f32[4,8,128]{2,1,0:T(8,128)S(1)}) custom-call(s32[8]{0:T(128)S(1)} %sub.29.nv_ref, f32[2,8,128]{2,1,0:T(8,128)S(1)} %broadcast_multiply_fusion.norm_ref, f32[12,128]{1,0:T(8,128)S(1)} %get-tuple-element.17.cos_ref, ...), custom_call_target="tpu_custom_call" | custom-call | tf_op jit(solution)/shard_map/pallas_call | solution.py:413
  132.6 0.0 copy-start
  132.6 1.8 %copy-done = bf16[4,4,2,112,512]{4,3,2,1,0:T(8,128)(2,1)} copy-done((bf16[4,4,2,112,512]{4,3,2,1,0:T(8,128)(2,1)}, bf16[4,4,2,112,512]{4,3,2,1,0:T(8,128)(2,1)S(1)}, u32[]{:S(2)}) %copy-start) | copy-done | bytes 3670040
  134.5 0.7 convert_element_type.53
  135.2 0.6 copy.21
  135.8 0.0 copy-start.1
  135.8 5.5 %copy.24 = bf16[3584,768]{1,0:T(8,128)(2,1)} copy(bf16[3584,768]{1,0:T(8,128)(2,1)} %bitcast.16) | data formatting | bytes 11010048
  141.3 0.0 copy-done.1
  141.3 1.8 %copy.25 = bf16[3584,512]{1,0:T(8,128)(2,1)} copy(bf16[3584,512]{1,0:T(8,128)(2,1)S(1)} %bitcast.14) | data formatting | bytes 7340032
  (9 shorter events, 0.1 us)
Async XLA Ops:
  6.7 1.1 copy-start.2
  7.8 1.0 copy-start.3
  132.6 1.8 %copy-start = (bf16[4,4,2,112,512]{4,3,2,1,0:T(8,128)(2,1)}, bf16[4,4,2,112,512]{4,3,2,1,0:T(8,128)(2,1)S(1)}, u32[]{:S(2)}) copy-start(bf16[4,4,2,112,512]{4,3,2,1,0:T(8,128)(2,1)S(1)} %get-tuple-element.11) | copy-start | bytes 11010052
  135.8 5.5 %copy-start.1 = (bf16[4,4,2,112,512]{4,3,2,1,0:T(8,128)(2,1)S(1)}, bf16[4,4,2,112,512]{4,3,2,1,0:T(8,128)(2,1)}, u32[]{:S(2)}) copy-start(bf16[4,4,2,112,512]{4,3,2,1,0:T(8,128)(2,1)} %copy-done) | copy-start | bytes 11010052

commit v2 on v1

--- a/solution.py
+++ b/solution.py
@@ -36,9 +36,9 @@
     nv_ref, norm_ref, cos_ref, sin_ref, bias_ref, wq_hbm, wo_hbm, k_hbm, v_hbm,
     sq, so, aout_ref, fkv_ref,
     wq, wo, kbuf, vbuf,
-    nbuf, pq, qred, qmine, qall, part, pred, attm, att, proj, gat,
+    nbuf, pq, qred, qmine, qall, part, pred, attm, att, proj, gat, fkv,
     loc_sem, kv_sem, own_sem,
-    a_send, a_recv, up_send, dn_send, z_recv, x_send, x_recv,
+    a_send, a_recv, up_send, dn_send, z_recv, x_send, x_recv, twin_send, twin_recv,
     n_send, n_recv, d1_send, d1_recv, d2_send, d2_recv, d3_send, d3_recv,
     d4_send, d4_recv, d5_send, d5_recv,
 ):
@@ -50,6 +50,8 @@
     rows = wq.shape[0]
     per = HQ // T
     QT = (HQ + 2 * KVH)
+    TWINS = (0, T - 1)
+    LATE = [i for i in range(T) if i not in TWINS] + list(TWINS)
     NC = nr * KVH
 
     def coords(i):
@@ -142,6 +144,9 @@
             wait_local(ref.at[z, s, x], a_recv.at[s, j])
         spread_own(s)
 
+    def crosses(zo, i):
+        return jnp.logical_not((zo == 0) | (zo == Z - 1)) if i in TWINS else zo >= 0
+
     def pass_on(k, i):
         s = lax.rem(tp + i, T)
 
@@ -149,8 +154,11 @@
         def _():
             for j, ref in both:
                 wait_local(ref.at[z - k, s, x], z_recv.at[z - k, s, j])
-                for dx in range(1, X):
-                    cross(dx, z - k, s, j, ref).start()
+
+                @pl.when(crosses(z - k, i))
+                def _():
+                    for dx in range(1, X):
+                        cross(dx, z - k, s, j, ref).start()
 
                 @pl.when(z + 1 < Z)
                 def _():
@@ -160,12 +168,54 @@
         def _():
             for j, ref in both:
                 wait_local(ref.at[z + k, s, x], z_recv.at[z + k, s, j])
-                for dx in range(1, X):
-                    cross(dx, z + k, s, j, ref).start()
+
+                @pl.when(crosses(z + k, i))
+                def _():
+                    for dx in range(1, X):
+                        cross(dx, z + k, s, j, ref).start()
 
                 @pl.when(z > 0)
                 def _():
                     down(z + k, s, j, ref).start()
+
+    def twin(dx, way, n, j, ref):
+        zo = (Z - 1) * way
+        piece = ref.at[zo, lax.rem(tp + TWINS[n], T), lax.rem(x + dx, X)]
+        nz = z - 1 if way else z + 1
+        return remote(piece, piece, twin_send.at[way, dx - 1, n, j], twin_recv.at[way, dx - 1, n, j], (nz, tp, x))
+
+    def each_twin():
+        for n in range(len(TWINS)):
+            for dx in range(1, X):
+                for j, ref in both:
+                    yield n, dx, j, ref
+
+    def twin_start():
+        for way in (0, 1):
+            zo = (Z - 1) * way
+
+            @pl.when(z == zo)
+            def _():
+                for n, dx, j, ref in each_twin():
+                    s, ox = lax.rem(tp + TWINS[n], T), lax.rem(x + dx, X)
+                    wait_local(ref.at[zo, s, ox], x_recv.at[ox, zo, s, j])
+                    twin(dx, way, n, j, ref).start()
+
+    def twin_pass(k):
+        for way in (0, 1):
+            zo = (Z - 1) * way
+
+            @pl.when((z + k == zo) if way else (z - k == zo))
+            def _():
+                for n, dx, j, ref in each_twin():
+                    s, ox = lax.rem(tp + TWINS[n], T), lax.rem(x + dx, X)
+                    wait_local(ref.at[zo, s, ox], twin_recv.at[way, dx - 1, n, j])
+                    if k < Z - 1:
+                        twin(dx, way, n, j, ref).start()
+
+    for j, ref in both:
+        wait_local(ref.at[z, tp, x], own_sem.at[j])
+    spread_own(tp)
 
     lhs = norm_ref[x]
     for dx in range(1, X):
@@ -202,9 +252,7 @@
             wait_local(buf.at[pl.ds(0, count)], ss)
 
     to_all(QT, lax.rem(me, QT), lambda j: pq.at[j], qred.at[me], d1_send, d1_recv)
-    for j, ref in both:
-        wait_local(ref.at[z, tp, x], own_sem.at[j])
-    spread_own(tp)
+    own_piece(1)
 
     @pl.when(me < QT)
     def _():
@@ -213,10 +261,10 @@
         qmine[...] = total.astype(jnp.bfloat16).astype(jnp.float32)
         to_all(ND, me, lambda j: qmine, qall.at[me], d2_send, d2_recv)
 
-    for dt in (1, 2):
-        if dt < T:
-            own_piece(dt)
+    for dt in range(2, T):
+        own_piece(dt)
     wait_local(qall, d2_recv)
+    twin_start()
 
     def turn(v, i):
         return v * cos_ref[i:i + 1, :] + pltpu.roll(v, HD // 2, 1) * sin_ref[i:i + 1, :]
@@ -241,12 +289,15 @@
         return out
 
     for r in range(nr):
+        if r % 2 == 0 and r // 2 < T:
+            pass_on(1, r // 2)
         mine = jnp.sum(jnp.where(sub3 == x * nr + r, everything, 0.0), axis=1)
         q = mine[:HQ]
         fk = turn(mine[HQ:HQ + KVH], r * (nb + 1) + nb).astype(jnp.bfloat16)
         fv = mine[HQ + KVH:]
-        fkv_ref[r, :KVH, :] = fk.astype(jnp.float32)
-        fkv_ref[r, KVH:, :] = fv
+        for g in range(KVH):
+            fkv[r:r + 1, g * HD:(g + 1) * HD] = fk.astype(jnp.float32)[g:g + 1]
+            fkv[r:r + 1, (KVH + g) * HD:(KVH + g + 1) * HD] = fv[g:g + 1]
         sqy = turn(q, r * (nb + 1) + nb).astype(jnp.bfloat16).astype(jnp.float32)
         own = scale * jnp.sum(sqy * per_head(fk.astype(jnp.float32)), axis=1, keepdims=True)
         own = jnp.where(first_dev, own, floor_score)
@@ -295,8 +346,11 @@
 
     lax.fori_loop(0, NC, to_group, 0)
 
-    for dt in range(3, T):
-        own_piece(dt)
+    for i in range(min(T, (nr + 1) // 2), T):
+        pass_on(1, i)
+    twin_pass(1)
+    for i in LATE[:T // 2]:
+        pass_on(2, i)
 
     @pl.when(gi < NC)
     def _():
@@ -311,8 +365,9 @@
         attm[...] = jnp.concatenate([val, jnp.zeros_like(val)], axis=0)
         to_all(ND, me, lambda j: attm, att.at[x * NC + gi], d4_send, d4_recv)
 
-    for i in range(T):
-        pass_on(1, i)
+    for i in LATE[T // 2:]:
+        pass_on(2, i)
+    twin_pass(2)
     wait_local(att, d4_recv)
 
     nrt = nr * X
@@ -328,15 +383,24 @@
         )
     proj[...] = jnp.zeros_like(proj)
     for i in range(nrt):
-        proj[i:i + 1, :rows] = jnp.sum(acc[i * SUB:(i + 1) * SUB], axis=0, keepdims=True)
-    to_all(ND, me, lambda j: proj, gat.at[me], d5_send, d5_recv)
-
-    for k in range(2, Z):
-        for i in range(T):
+        proj[i // nr, i % nr:i % nr + 1, :rows] = jnp.sum(acc[i * SUB:(i + 1) * SUB], axis=0, keepdims=True)
+    to_all(ND, me, lambda j: proj.at[lax.rem(j, X)], gat.at[me], d5_send, d5_recv)
+
+    for k in range(3, Z):
+        for i in LATE:
             pass_on(k, i)
+        twin_pass(k)
 
     wait_local(gat, d5_recv)
-    aout_ref[...] = gat[...]
+    lane1 = lax.broadcasted_iota(jnp.int32, (SUB, LANES), 1)
+    for t in range(ND * rows // LANES):
+        row = jnp.zeros((SUB, LANES), jnp.float32)
+        for d in range(t * LANES // rows, ((t + 1) * LANES - 1) // rows + 1):
+            off = d * rows - t * LANES
+            moved = gat[d] if off == 0 else pltpu.roll(gat[d], off % LANES, 1)
+            row = jnp.where((lane1 >= off) & (lane1 < off + rows), moved, row)
+        aout_ref[:, t * LANES:(t + 1) * LANES] = row[:nr].astype(jnp.bfloat16)
+    fkv_ref[...] = fkv[:nr].astype(jnp.bfloat16)
 
     for dx in range(1, X):
         norm_copy(dx).wait_send()
@@ -370,13 +434,29 @@
             def _():
                 wait_local(piece, dn_send.at[zo, s, j])
 
-            for dx in range(1, X):
-                wait_local(piece, x_send.at[dx - 1, zo, s, j])
-                ox = lax.rem(x + dx, X)
-                wait_local(ref.at[zo, s, ox], x_recv.at[ox, zo, s, j])
+            i = lax.rem(s - tp + T, T)
+            twinned = ((i == TWINS[0]) | (i == TWINS[1])) & ((zo == 0) | (zo == Z - 1))
+
+            @pl.when(jnp.logical_not(twinned) | (zo == z))
+            def _():
+                for dx in range(1, X):
+                    wait_local(piece, x_send.at[dx - 1, zo, s, j])
+
+            @pl.when(jnp.logical_not(twinned))
+            def _():
+                for dx in range(1, X):
+                    ox = lax.rem(x + dx, X)
+                    wait_local(ref.at[zo, s, ox], x_recv.at[ox, zo, s, j])
+
         return c
 
     lax.fori_loop(0, Z * T, finish, 0)
+
+    for way in (0, 1):
+        @pl.when((z > 0) if way else (z + 1 < Z))
+        def _():
+            for n, dx, j, ref in each_twin():
+                wait_local(ref.at[z, tp, x], twin_send.at[way, dx - 1, n, j])
 
 
 def make_body(Z, T, X):
@@ -410,15 +490,15 @@
         dma = pltpu.SemaphoreType.DMA
         f32, bf = jnp.float32, jnp.bfloat16
         tile = (SUB, LANES)
-        sq, so, gat, fkv = pl.pallas_call(
+        sq, so, attended, fresh_kv = pl.pallas_call(
             functools.partial(kernel, Z, T, X, nr, nb),
             out_shape=(
                 jax.ShapeDtypeStruct((Z, T, X, rows, SC), bf),
                 jax.ShapeDtypeStruct((Z, T, X, rows, HW), bf),
-                jax.ShapeDtypeStruct((ND,) + tile, f32),
-                jax.ShapeDtypeStruct((nr, 2 * KVH, HD), f32),
+                jax.ShapeDtypeStruct((nr, D), bf),
+                jax.ShapeDtypeStruct((nr, 2 * KVH * HD), bf),
             ),
-            in_specs=[pl.BlockSpec(memory_space=pltpu.SMEM)] + [vm] * 4 + [anys] * 4,
+            in_specs=[pl.BlockSpec(memory_space=pltpu.SMEM)] + [vm] * 4 + [pl.BlockSpec(memory_space=pltpu.HBM)] * 4,
             out_specs=(anys, anys, vm, vm),
             scratch_shapes=[
                 pltpu.VMEM(qkv_weight.shape, bf),
@@ -434,21 +514,21 @@
                 pltpu.VMEM((NG,) + tile, f32),
                 pltpu.VMEM(tile, f32),
                 pltpu.VMEM((X * NC,) + tile, f32),
-                pltpu.VMEM(tile, f32),
+                pltpu.VMEM((X,) + tile, f32),
                 pltpu.VMEM((ND,) + tile, f32),
+                pltpu.VMEM((SUB, 2 * KVH * HD), f32),
                 dma((2,)), dma((2,)), dma((2,)),
                 dma((T, 2)), dma((T, 2)),
                 dma((Z, T, 2)), dma((Z, T, 2)), dma((Z, T, 2)),
                 dma((X - 1, Z, T, 2)), dma((X, Z, T, 2)),
+                dma((2, X - 1, 2, 2)), dma((2, X - 1, 2, 2)),
                 dma((X - 1,)), dma((X,)),
             ] + [dma] * 10,
             compiler_params=pltpu.CompilerParams(
-                collective_id=0, has_side_effects=True, vmem_limit_bytes=48 * 1024 * 1024
+                collective_id=0, has_side_effects=True, vmem_limit_bytes=26 * 1024 * 1024
             ),
-        )(nv, blocks, cos2, sin2, bias, qkv_weight, out_weight, key_cache, value_cache)
-        mine = lax.dynamic_slice_in_dim(gat, x * nr, nr, 1)[:, :, :rows]
-        attended = mine.transpose(1, 0, 2).reshape(nr, D).astype(bf)
-        fresh_kv = fkv.reshape(nr, 2 * KVH * HD).astype(bf)
+        )(nv, blocks, cos2, sin2, bias, *(
+            pltpu.with_memory_space_constraint(a, pltpu.HBM) for a in (qkv_weight, out_weight, key_cache, value_cache)))
         return attended, fresh_kv, sq.reshape(D, SC), so.reshape(D, HW)
 
     return body

time: 144 us -> 124 us (0.86)
  Pallas kernels: 124 us -> 111 us
  local copies, waits for them, and re-layouts: 13.9 us -> 6.77 us
    pallas_call x1, Pallas kernels: 124 us -> 111 us  [body(): pl.pallas_call(functools.partial(kernel, Z, T, X, nr, nb), out_shape=(jax...]
    unnamed x12 -> x5, local copies, waits for them, and re-layouts: 11.9 us -> 5.49 us
where the time goes in v2:
time: 124 us
  Pallas kernels  111 us (90%)
  local copies, waits for them, and re-layouts  6.77 us (5%)
  other arithmetic  4.79 us (4%)
    pallas_call x1, Pallas kernels, body(): pl.pallas_call(functools.partial(kernel, Z, T, X, nr, nb), out_shape=(jax...  111 us
    unnamed x5, local copies, waits for them, and re-layouts  5.49 us

profile of v2, /device:TPU:0, one launch (start us, length us, event | category | flops | bytes accessed | tf_op | source)
XLA Modules:
  0.0 123.6 jit_solution(8190962847048987479)
XLA Ops:
  0.6 0.1 mul.74
  0.7 0.1 mul.75
  0.8 0.9 multiply_reduce_fusion
  1.7 0.7 fusion.4
  2.4 0.8 dynamic-slice
  3.1 0.7 add_convert_fusion
  3.8 0.1 copy.16
  3.9 0.1 convert_element_type.38
  4.0 0.1 broadcast_subtract_fusion
  4.1 0.1 sub.29.nv_ref
  4.2 0.7 reshape.64
  4.9 0.8 fusion.2
  5.6 0.1 pad_maximum_fusion
  5.7 0.8 convert_element_type.33
  6.5 0.1 fusion.3
  6.6 0.1 reshape.59
  6.7 0.1 broadcast_multiply_fusion.norm_ref
  6.7 111.3 %shard_map.129 = (bf16[4,4,2,112,768]{4,3,2,1,0:T(8,128)(2,1)S(1)}, bf16[4,4,2,112,512]{4,3,2,1,0:T(8,128)(2,1)S(1)}, bf16[4,3584]{1,0:T(4,128)(2,1)S(1)}, bf16[4,1024]{1,0:T(4,128)(2,1)S(1)}) custom-call(s32[8]{0:T(128)S(1)} %sub.29.nv_ref, f32[2,8,128]{2,1,0:T(8,128)S(1)} %broadcast_multiply_fusion.norm_ref, f32[12,128]{1,0:T(8,128)S(1)} %get-tuple-element.17.cos_ref, ...), custom_call_target="tpu_custom_call" | custom-call | tf_op jit(solution)/shard_map/pallas_call | solution.py:493
  118.1 0.6 copy.22
  118.7 0.6 copy.23
  119.3 2.4 %copy.24 = bf16[3584,768]{1,0:T(8,128)(2,1)} copy(bf16[3584,768]{1,0:T(8,128)(2,1)S(1)} %bitcast.7) | data formatting | bytes 11010048
  121.7 1.8 %copy.25 = bf16[3584,512]{1,0:T(8,128)(2,1)} copy(bf16[3584,512]{1,0:T(8,128)(2,1)S(1)} %bitcast.8) | data formatting | bytes 7340032
  (6 shorter events, 0.0 us)

commit v3 on v2

--- a/solution.py
+++ b/solution.py
@@ -257,7 +257,7 @@
     @pl.when(me < QT)
     def _():
         wait_local(qred, d1_recv)
-        total = jnp.sum(qred[...], axis=0) + bias_ref[me]
+        total = jnp.sum(qred[...], axis=0) + bias_ref[:, pl.ds(pl.multiple_of(me * HD, LANES), HD)].astype(jnp.float32)
         qmine[...] = total.astype(jnp.bfloat16).astype(jnp.float32)
         to_all(ND, me, lambda j: qmine, qall.at[me], d2_send, d2_recv)
 
@@ -484,7 +484,7 @@
         sin2 = jnp.concatenate([-sine, sine], axis=1)
         start = (z * T + tp) * key_cache.shape[1]
         nv = (cache_len[:, None] - start - BLOCK * jnp.arange(nb, dtype=jnp.int32)[None]).reshape(-1)
-        bias = qkv_bias.astype(jnp.float32).reshape(QT, 1, HD)
+        bias = qkv_bias.reshape(1, QT * HD)
         vm = pl.BlockSpec(memory_space=pltpu.VMEM)
         anys = pl.BlockSpec(memory_space=pl.ANY)
         dma = pltpu.SemaphoreType.DMA

time: 124 us -> 124 us (level)
  no operation moved by 1% of the time
where the time goes in v3:
time: 124 us
  Pallas kernels  111 us (90%)
  local copies, waits for them, and re-layouts  7.48 us (6%)
  other arithmetic  4.09 us (3%)
    pallas_call x1, Pallas kernels, body(): pl.pallas_call(functools.partial(kernel, Z, T, X, nr, nb), out_shape=(jax...  111 us
    unnamed x5, local copies, waits for them, and re-layouts  5.49 us

profile of v3, /device:TPU:0, one launch (start us, length us, event | category | flops | bytes accessed | tf_op | source)
XLA Modules:
  0.0 123.6 jit_solution(2393850088058558937)
XLA Ops:
  0.6 0.1 mul.74
  0.7 0.1 mul.75
  0.8 0.9 multiply_reduce_fusion
  1.7 0.7 fusion.4
  2.4 0.8 dynamic-slice
  3.1 0.7 add_convert_fusion
  3.8 0.1 copy.16
  3.9 0.1 convert_element_type.37
  4.0 0.1 broadcast_subtract_fusion
  4.1 0.1 sub.29.nv_ref
  4.2 0.7 reshape.58.bias_ref
  4.9 0.8 fusion.2
  5.6 0.1 pad_maximum_fusion
  5.7 0.8 convert_element_type.32
  6.5 0.1 fusion.3
  6.6 0.1 reshape.57
  6.7 0.1 broadcast_multiply_fusion.norm_ref
  6.7 111.3 %shard_map.129 = (bf16[4,4,2,112,768]{4,3,2,1,0:T(8,128)(2,1)S(1)}, bf16[4,4,2,112,512]{4,3,2,1,0:T(8,128)(2,1)S(1)}, bf16[4,3584]{1,0:T(4,128)(2,1)S(1)}, bf16[4,1024]{1,0:T(4,128)(2,1)S(1)}) custom-call(s32[8]{0:T(128)S(1)} %sub.29.nv_ref, f32[2,8,128]{2,1,0:T(8,128)S(1)} %broadcast_multiply_fusion.norm_ref, f32[12,128]{1,0:T(8,128)S(1)} %get-tuple-element.17.cos_ref, ...), custom_call_target="tpu_custom_call" | custom-call | tf_op jit(solution)/shard_map/pallas_call | solution.py:493
  118.1 0.6 copy.22
  118.7 0.6 copy.23
  119.3 2.4 %copy.24 = bf16[3584,768]{1,0:T(8,128)(2,1)} copy(bf16[3584,768]{1,0:T(8,128)(2,1)S(1)} %bitcast.6) | data formatting | bytes 11010048
  121.7 1.8 %copy.25 = bf16[3584,512]{1,0:T(8,128)(2,1)} copy(bf16[3584,512]{1,0:T(8,128)(2,1)S(1)} %bitcast.7) | data formatting | bytes 7340032
  (6 shorter events, 0.0 us)
